TPU v7x, 32 devices: a whole 2x2x4 slice. The times are simulated.
32 devices in a mesh: gx: 2 (over x), gy: 4 (over y, core), gz: 4 (over z).
Axes of the slice: x: 2, y: 2, z: 4, core: 2. Of those that a mesh axis runs over, the one named last changes fastest.
Arguments:
- dual_rhs: float32 [2, 4, 4, 3, 300, 128], P('gx', 'gy', 'gz'), may hold values from -6 to 6
- local_flex: bfloat16 [2, 4, 4, 1800, 1800], P('gx', 'gy', 'gz'), as said below
- corner_coupling: bfloat16 [2, 4, 4, 24, 1800], P('gx', 'gy', 'gz'), may hold values from -0.375 to 0.375
- face_stiffness: bfloat16 [2, 4, 4, 6, 300, 300], P('gx', 'gy', 'gz'), as said below
- coarse_inverse: bfloat16 [27, 27], replicated, as said below
- corner_ids: int32 [2, 4, 4, 8], P('gx', 'gy', 'gz'), may hold values from -1 to 8, as said below
Outputs:
- multipliers: float32 [2, 4, 4, 3, 300, 128], P('gx', 'gy', 'gz')
- residual: float32 [2, 4, 4, 3, 300, 128], P('gx', 'gy', 'gz')
Inputs may be any that keep to these rules, and one draw needn't show every extreme that they name: `local_flex`: each subdomain's matrix is symmetric positive definite. `face_stiffness`: each face block is symmetric positive definite. `coarse_inverse`: symmetric positive definite. `corner_ids`: entry k = 4 kx + 2 ky + kz of subdomain (i, j, l) is the number of the corner at lattice point (i + kx, j + ky, l + kz) when that point has all coordinates strictly between 0 and the subdomain counts, else -1; the 9 interior corners are numbered by a permutation, so subdomains sharing a corner name the same node.
All inputs are finite; a program needn't handle non-finite values.
Results may differ from a plain program's by a relative error of at most 0.04.
Values may be sent and summed in bfloat16 or wider, within the bound.
A program may use at most 64 MiB of HBM per device.

v0:
```python
import jax
import jax.numpy as jnp
from jax import lax
from jax.sharding import PartitionSpec as P

ITERS = 3


def with_halo(value, sides, width):
    for axis, dim in sides:
        size, length = (lax.axis_size(axis), value.shape[dim])
        up = [(i, (i + 1) % size) for i in range(size - 1)]
        down = [(j, i) for i, j in up]
        last = lax.slice_in_dim(value, length - width, length, axis=dim)
        first = lax.slice_in_dim(value, 0, width, axis=dim)
        before = lax.ppermute(last, axis, up)
        after = lax.ppermute(first, axis, down)
        value = jnp.concatenate([before, value, after], axis=dim)
    return value


def face_neighbours(face_pairs):
    along_x = with_halo(face_pairs[0].astype(jnp.bfloat16), (("gx", 0),), 1).astype(jnp.float32)
    along_y = with_halo(face_pairs[1].astype(jnp.bfloat16), (("gy", 0),), 1).astype(jnp.float32)
    along_z = with_halo(face_pairs[2].astype(jnp.bfloat16), (("gz", 0),), 1).astype(jnp.float32)
    return [along_x, along_y, along_z]


def face_jump(values, face_mask):
    extended = face_neighbours([values[0:2], values[2:4], values[4:6]])
    face_list = []
    for bordered in extended:
        face_list.append(bordered[0] - bordered[1])
        face_list.append(bordered[2] - bordered[3])
    return jnp.stack(face_list) * face_mask[:, None, None]


def duplicate(owned, face_mask):
    empty = jnp.zeros_like(owned[0])
    extended = face_neighbours([jnp.stack([empty, owned[axis_pos]]) for axis_pos in range(3)])
    face_list = []
    for axis_pos in range(3):
        face_list.append(extended[axis_pos][0])
        face_list.append(owned[axis_pos])
    return jnp.stack(face_list) * face_mask[:, None, None]


def owned_inner(left, right):
    return jnp.sum(left[1::2] * right[1::2], axis=(0, 1))


def body(dual_rhs, local_flex, corner_coupling, face_stiffness, coarse_inverse, corner_ids):
    owned_rhs = dual_rhs[0, 0, 0]
    flex = local_flex[0, 0, 0]
    coupling = corner_coupling[0, 0, 0]
    stiffness = face_stiffness[0, 0, 0]
    corner_list = corner_ids[0, 0, 0]
    face_count, face_width, columns = (stiffness.shape[0], stiffness.shape[1], owned_rhs.shape[2])
    coarse_rows = coarse_inverse.shape[0]
    face_sign = jnp.array([-1.0, 1.0, -1.0, 1.0, -1.0, 1.0], jnp.float32)[:, None, None]
    place_x = lax.axis_index("gx")
    place_y = lax.axis_index("gy")
    place_z = lax.axis_index("gz")
    face_mask = jnp.stack(
        [
            place_x > 0,
            place_x < lax.axis_size("gx") - 1,
            place_y > 0,
            place_y < lax.axis_size("gy") - 1,
            place_z > 0,
            place_z < lax.axis_size("gz") - 1,
        ]
    ).astype(jnp.float32)
    coupling_wide = coupling.astype(jnp.float32)
    dof_ids = jnp.where(
        corner_list[:, None] >= 0,
        3 * corner_list[:, None] + jnp.arange(3, dtype=jnp.int32)[None, :],
        -1,
    ).reshape(-1)
    assembly = (jnp.arange(coarse_rows, dtype=jnp.int32)[:, None] == dof_ids[None, :]).astype(
        jnp.float32
    )

    def precondition(dual):
        halved = (0.5 * face_sign * dual).astype(jnp.bfloat16)
        own_part = jnp.einsum("fij,fjr->fir", stiffness, halved, preferred_element_type=jnp.float32)
        return 0.5 * face_jump(own_part, face_mask)

    def local_terms(direction):
        signed = (
            (face_sign * direction).astype(jnp.bfloat16).reshape(face_count * face_width, columns)
        )
        local_image = jnp.dot(flex, signed, preferred_element_type=jnp.float32)
        corner_part = jnp.dot(coupling, signed, preferred_element_type=jnp.float32)
        coarse_part = jnp.dot(assembly, corner_part, precision=lax.Precision.HIGHEST)
        return (signed, local_image, coarse_part)

    def finish(local_image, coarse_rhs):
        coarse_sol = jnp.dot(
            coarse_inverse, coarse_rhs.astype(jnp.bfloat16), preferred_element_type=jnp.float32
        )
        corner_sol = lax.dot_general(
            assembly, coarse_sol, (((0,), (0,)), ((), ())), precision=lax.Precision.HIGHEST
        )
        displaced = local_image + lax.dot_general(
            coupling_wide, corner_sol, (((0,), (0,)), ((), ())), precision=lax.Precision.HIGHEST
        )
        return (coarse_sol, displaced)

    residual = duplicate(owned_rhs, face_mask)
    multiplier = jnp.zeros_like(residual)

    def merged_operator(precond_res, current):
        signed, local_image, coarse_part = local_terms(precond_res)
        energy_local = jnp.sum(signed.astype(jnp.float32) * local_image, axis=0)
        coarse_rhs, rho_sum, energy_sum = lax.psum(
            (coarse_part, owned_inner(current, precond_res), energy_local), ("gx", "gy", "gz")
        )
        coarse_sol, displaced = finish(local_image, coarse_rhs)
        energy = energy_sum + jnp.sum(coarse_rhs * coarse_sol, axis=0)
        image = face_jump(displaced.reshape(face_count, face_width, columns), face_mask)
        return (image, rho_sum, energy)

    precond_res = precondition(residual)
    precond_image, rho_now, energy = merged_operator(precond_res, residual)
    step_size = rho_now / energy
    direction = precond_res
    direction_image = precond_image
    for iteration in range(ITERS):
        multiplier = multiplier + step_size * direction
        residual = residual - step_size * direction_image
        if iteration + 1 < ITERS:
            precond_res = precondition(residual)
            precond_image, rho_next, energy = merged_operator(precond_res, residual)
            beta_now = rho_next / rho_now
            next_step = rho_next / (energy - beta_now * rho_next / step_size)
            direction = precond_res + beta_now * direction
            direction_image = precond_image + beta_now * direction_image
            rho_now = rho_next
            step_size = next_step
    return (multiplier[1::2][None, None, None], residual[1::2][None, None, None])


def solution(mesh):
    placed = (
        P("gx", "gy", "gz", None, None, None),
        P("gx", "gy", "gz", None, None),
        P("gx", "gy", "gz", None, None),
        P("gx", "gy", "gz", None, None, None),
        P(),
        P("gx", "gy", "gz", None),
    )
    return jax.shard_map(
        body,
        mesh=mesh,
        in_specs=placed,
        out_specs=(P("gx", "gy", "gz", None, None, None), P("gx", "gy", "gz", None, None, None)),
        check_vma=False,
    )
```

profile of v0, /device:TPU:0, one launch (start us, length us, event | category | flops | bytes accessed | tf_op | source)
XLA Modules:
  0.0 316.8 jit_solution(4890073381074948093)
XLA Ops:
  1.9 4.9 %collective-permute-start = (bf16[1,300,128]{2,1,0:T(8,128)(2,1)S(1)}, bf16[1,300,128]{2,1,0:T(8,128)(2,1)S(1)}, u32[]{:S(2)}, u32[]{:S(2)}) collective-permute-start(bf16[1,300,128]{2,1,0:T(8,128)(2,1)S(1)} %bitcast.178), channel_id=1, source_target_pairs={{0,16},{1,17},{2,18},{3,19},{4,20},{5,21},{6,22},{7,23},{8,24},{9,... | collective-permute-start | bytes 230408 | tf_op jit(solution)/shard_map/ppermute | solution.py:16
  8.3 3.5 %collective-permute-start.2 = (bf16[1,300,128]{2,1,0:T(8,128)(2,1)S(1)}, bf16[1,300,128]{2,1,0:T(8,128)(2,1)S(1)}, u32[]{:S(2)}, u32[]{:S(2)}) collective-permute-start(bf16[1,300,128]{2,1,0:T(8,128)(2,1)S(1)} %bitcast.176), channel_id=1, source_target_pairs={{0,1},{1,2},{2,3},{4,5},{5,6},{6,7},{8,9},{9,10},{10,11},{12,13},{... | collective-permute-start | bytes 230408 | tf_op jit(solution)/shard_map/ppermute | solution.py:16
  18.2 4.6 %collective-permute-start.3 = (bf16[1,300,128]{2,1,0:T(8,128)(2,1)S(1)}, bf16[1,300,128]{2,1,0:T(8,128)(2,1)S(1)}, u32[]{:S(2)}, u32[]{:S(2)}) collective-permute-start(bf16[1,300,128]{2,1,0:T(8,128)(2,1)S(1)} %get-tuple-element.53), channel_id=1, source_target_pairs={{0,16},{1,17},{2,18},{3,19},{4,20},{5,21},{6,22},{7,23},{8,24},{9,... | collective-permute-start | bytes 230408 | tf_op jit(solution)/shard_map/ppermute | solution.py:16
  24.1 3.8 %collective-permute-start.5 = (bf16[1,300,128]{2,1,0:T(8,128)(2,1)S(1)}, bf16[1,300,128]{2,1,0:T(8,128)(2,1)S(1)}, u32[]{:S(2)}, u32[]{:S(2)}) collective-permute-start(bf16[1,300,128]{2,1,0:T(8,128)(2,1)S(1)} %get-tuple-element.51), channel_id=1, source_target_pairs={{0,4},{4,8},{8,12},{1,5},{5,9},{9,13},{2,6},{6,10},{10,14},{3,7},{... | collective-permute-start | bytes 230408 | tf_op jit(solution)/shard_map/ppermute | solution.py:16
  29.2 4.6 %collective-permute-start.7 = (bf16[1,300,128]{2,1,0:T(8,128)(2,1)S(1)}, bf16[1,300,128]{2,1,0:T(8,128)(2,1)S(1)}, u32[]{:S(2)}, u32[]{:S(2)}) collective-permute-start(bf16[1,300,128]{2,1,0:T(8,128)(2,1)S(1)} %get-tuple-element.48), channel_id=1, source_target_pairs={{0,1},{1,2},{2,3},{4,5},{5,6},{6,7},{8,9},{9,10},{10,11},{12,13},{... | collective-permute-start | bytes 230408 | tf_op jit(solution)/shard_map/ppermute | solution.py:16
  39.3 5.4 %fusion.6 = f32[1800,128]{1,0:T(8,128)S(1)} fusion(bf16[1800,128]{1,0:T(8,128)(2,1)} %convert_element_type.206, bf16[1,1,1,1800,1800]{4,3,2,1,0:T(8,128)(2,1)} %param.8), kind=kOutput, calls=%fused_computation.6 | convolution fusion | flops 829440000 | bytes 7862400 | tf_op jit(solution)/shard_map/dot_general | solution.py:93
  46.0 40.6 %all-reduce.2 = (f32[27,128]{1,0:T(8,128)S(1)}, f32[128]{0:T(128)S(1)}, f32[128]{0:T(128)S(1)}) all-reduce(f32[27,128]{1,0:T(8,128)S(1)} %fusion.107, f32[128]{0:T(128)S(1)} %multiply_reduce_fusion.5, f32[128]{0:T(128)S(1)} %multiply_reduce_fusion.2), channel_id=1, replica_groups=mesh['gx'=2,'gy'=4,'gz'=4] {'gx','gy','gz'}, use_global_device_ids=true, to_apply=%region_4.5 | all-reduce | flops 3712 | bytes 29696 | tf_op jit(solution)/shard_map/psum | solution.py:116
  89.3 4.6 %collective-permute-start.9 = (bf16[1,300,128]{2,1,0:T(8,128)(2,1)S(1)}, bf16[1,300,128]{2,1,0:T(8,128)(2,1)S(1)}, u32[]{:S(2)}, u32[]{:S(2)}) collective-permute-start(bf16[1,300,128]{2,1,0:T(8,128)(2,1)S(1)} %get-tuple-element.80), channel_id=1, source_target_pairs={{0,16},{1,17},{2,18},{3,19},{4,20},{5,21},{6,22},{7,23},{8,24},{9,... | collective-permute-start | bytes 230408 | tf_op jit(solution)/shard_map/ppermute | solution.py:16
  95.2 3.0 collective-permute-start.11
  100.2 4.6 %collective-permute-start.13 = (bf16[1,300,128]{2,1,0:T(8,128)(2,1)S(1)}, bf16[1,300,128]{2,1,0:T(8,128)(2,1)S(1)}, u32[]{:S(2)}, u32[]{:S(2)}) collective-permute-start(bf16[1,300,128]{2,1,0:T(8,128)(2,1)S(1)} %get-tuple-element.75), channel_id=1, source_target_pairs={{0,1},{1,2},{2,3},{4,5},{5,6},{6,7},{8,9},{9,10},{10,11},{12,13},{... | collective-permute-start | bytes 230408 | tf_op jit(solution)/shard_map/ppermute | solution.py:16
  105.0 1.8 collective-permute-done.13
  111.2 4.6 %collective-permute-start.15 = (bf16[1,300,128]{2,1,0:T(8,128)(2,1)S(1)}, bf16[1,300,128]{2,1,0:T(8,128)(2,1)S(1)}, u32[]{:S(2)}, u32[]{:S(2)}) collective-permute-start(bf16[1,300,128]{2,1,0:T(8,128)(2,1)S(1)} %get-tuple-element.44), channel_id=1, source_target_pairs={{0,16},{1,17},{2,18},{3,19},{4,20},{5,21},{6,22},{7,23},{8,24},{9,... | collective-permute-start | bytes 230408 | tf_op jit(solution)/shard_map/ppermute | solution.py:16
  117.1 3.0 collective-permute-start.17
  121.4 5.2 %collective-permute-start.19 = (bf16[1,300,128]{2,1,0:T(8,128)(2,1)S(1)}, bf16[1,300,128]{2,1,0:T(8,128)(2,1)S(1)}, u32[]{:S(2)}, u32[]{:S(2)}) collective-permute-start(bf16[1,300,128]{2,1,0:T(8,128)(2,1)S(1)} %get-tuple-element.39), channel_id=1, source_target_pairs={{0,1},{1,2},{2,3},{4,5},{5,6},{6,7},{8,9},{9,10},{10,11},{12,13},{... | collective-permute-start | bytes 230408 | tf_op jit(solution)/shard_map/ppermute | solution.py:16
  131.0 1.9 convert_element_type.221
  132.9 5.3 %fusion.9 = f32[1800,128]{1,0:T(8,128)S(1)} fusion(bf16[1800,128]{1,0:T(8,128)(2,1)} %convert_element_type.221, bf16[1,1,1,1800,1800]{4,3,2,1,0:T(8,128)(2,1)} %param.8), kind=kOutput, calls=%fused_computation.7 | convolution fusion | flops 829440000 | bytes 7862400 | tf_op jit(solution)/shard_map/dot_general | solution.py:93
  139.7 41.2 %all-reduce.1 = (f32[128]{0:T(128)S(1)}, f32[128]{0:T(128)S(1)}, f32[27,128]{1,0:T(8,128)S(1)}) all-reduce(f32[128]{0:T(128)S(1)} %multiply_reduce_fusion.4, f32[128]{0:T(128)S(1)} %multiply_reduce_fusion.1, f32[27,128]{1,0:T(8,128)S(1)} %fusion.105), channel_id=1, replica_groups=mesh['gx'=2,'gy'=4,'gz'=4] {'gx','gy','gz'}, use_global_device_ids=true, to_apply=%region_7.8 | all-reduce | flops 3712 | bytes 29696 | tf_op jit(solution)/shard_map/psum | solution.py:116
  181.3 2.1 fusion.19
  186.0 5.8 %collective-permute-start.21 = (bf16[1,300,128]{2,1,0:T(8,128)(2,1)S(1)}, bf16[1,300,128]{2,1,0:T(8,128)(2,1)}, u32[]{:S(2)}, u32[]{:S(2)}) collective-permute-start(bf16[1,300,128]{2,1,0:T(8,128)(2,1)S(1)} %get-tuple-element.71), channel_id=1, source_target_pairs={{0,16},{1,17},{2,18},{3,19},{4,20},{5,21},{6,22},{7,23},{8,24},{9,... | collective-permute-start | bytes 230408 | tf_op jit(solution)/shard_map/ppermute | solution.py:16
  193.1 3.7 %collective-permute-start.23 = (bf16[1,300,128]{2,1,0:T(8,128)(2,1)S(1)}, bf16[1,300,128]{2,1,0:T(8,128)(2,1)}, u32[]{:S(2)}, u32[]{:S(2)}) collective-permute-start(bf16[1,300,128]{2,1,0:T(8,128)(2,1)S(1)} %get-tuple-element.69), channel_id=1, source_target_pairs={{0,4},{4,8},{8,12},{1,5},{5,9},{9,13},{2,6},{6,10},{10,14},{3,7},{... | collective-permute-start | bytes 230408 | tf_op jit(solution)/shard_map/ppermute | solution.py:16
  199.5 4.6 %collective-permute-start.25 = (bf16[1,300,128]{2,1,0:T(8,128)(2,1)S(1)}, bf16[1,300,128]{2,1,0:T(8,128)(2,1)S(1)}, u32[]{:S(2)}, u32[]{:S(2)}) collective-permute-start(bf16[1,300,128]{2,1,0:T(8,128)(2,1)S(1)} %get-tuple-element.66), channel_id=1, source_target_pairs={{0,1},{1,2},{2,3},{4,5},{5,6},{6,7},{8,9},{9,10},{10,11},{12,13},{... | collective-permute-start | bytes 230408 | tf_op jit(solution)/shard_map/ppermute | solution.py:16
  211.2 4.6 %collective-permute-start.27 = (bf16[1,300,128]{2,1,0:T(8,128)(2,1)S(1)}, bf16[1,300,128]{2,1,0:T(8,128)(2,1)S(1)}, u32[]{:S(2)}, u32[]{:S(2)}) collective-permute-start(bf16[1,300,128]{2,1,0:T(8,128)(2,1)S(1)} %get-tuple-element.35), channel_id=1, source_target_pairs={{0,16},{1,17},{2,18},{3,19},{4,20},{5,21},{6,22},{7,23},{8,24},{9,... | collective-permute-start | bytes 230408 | tf_op jit(solution)/shard_map/ppermute | solution.py:16
  217.1 3.0 collective-permute-start.29
  221.4 5.0 %collective-permute-start.31 = (bf16[1,300,128]{2,1,0:T(8,128)(2,1)S(1)}, bf16[1,300,128]{2,1,0:T(8,128)(2,1)S(1)}, u32[]{:S(2)}, u32[]{:S(2)}) collective-permute-start(bf16[1,300,128]{2,1,0:T(8,128)(2,1)S(1)} %get-tuple-element.30), channel_id=1, source_target_pairs={{0,1},{1,2},{2,3},{4,5},{5,6},{6,7},{8,9},{9,10},{10,11},{12,13},{... | collective-permute-start | bytes 230408 | tf_op jit(solution)/shard_map/ppermute | solution.py:16
  231.5 1.9 convert_element_type.236
  233.4 5.3 %fusion.12 = f32[1800,128]{1,0:T(8,128)S(1)} fusion(bf16[1800,128]{1,0:T(8,128)(2,1)} %convert_element_type.236, bf16[1,1,1,1800,1800]{4,3,2,1,0:T(8,128)(2,1)} %param.8), kind=kOutput, calls=%fused_computation.8 | convolution fusion | flops 829440000 | bytes 7862400 | tf_op jit(solution)/shard_map/dot_general | solution.py:93
  240.3 41.5 %all-reduce = (f32[128]{0:T(128)S(1)}, f32[128]{0:T(128)}, f32[27,128]{1,0:T(8,128)S(1)}) all-reduce(f32[128]{0:T(128)S(1)} %multiply_reduce_fusion.3, f32[128]{0:T(128)S(1)} %multiply_reduce_fusion, f32[27,128]{1,0:T(8,128)S(1)} %fusion.103), channel_id=1, replica_groups=mesh['gx'=2,'gy'=4,'gz'=4] {'gx','gy','gz'}, use_global_device_ids=true, to_apply=%region_13.14 | all-reduce | flops 3712 | bytes 29696 | tf_op jit(solution)/shard_map/psum | solution.py:116
  282.1 2.1 fusion.20
  287.0 5.8 %collective-permute-start.33 = (bf16[1,300,128]{2,1,0:T(8,128)(2,1)}, bf16[1,300,128]{2,1,0:T(8,128)(2,1)}, u32[]{:S(2)}, u32[]{:S(2)}) collective-permute-start(bf16[1,300,128]{2,1,0:T(8,128)(2,1)} %get-tuple-element.62), channel_id=1, source_target_pairs={{0,16},{1,17},{2,18},{3,19},{4,20},{5,21},{6,22},{7,23},{8,24},{9,... | collective-permute-start | bytes 230408 | tf_op jit(solution)/shard_map/ppermute | solution.py:16
  294.1 3.7 %collective-permute-start.35 = (bf16[1,300,128]{2,1,0:T(8,128)(2,1)}, bf16[1,300,128]{2,1,0:T(8,128)(2,1)}, u32[]{:S(2)}, u32[]{:S(2)}) collective-permute-start(bf16[1,300,128]{2,1,0:T(8,128)(2,1)} %get-tuple-element.60), channel_id=1, source_target_pairs={{0,4},{4,8},{8,12},{1,5},{5,9},{9,13},{2,6},{6,10},{10,14},{3,7},{... | collective-permute-start | bytes 230408 | tf_op jit(solution)/shard_map/ppermute | solution.py:16
  303.0 4.6 %collective-permute-start.37 = (bf16[1,300,128]{2,1,0:T(8,128)(2,1)S(1)}, bf16[1,300,128]{2,1,0:T(8,128)(2,1)S(1)}, u32[]{:S(2)}, u32[]{:S(2)}) collective-permute-start(bf16[1,300,128]{2,1,0:T(8,128)(2,1)S(1)} %get-tuple-element.57), channel_id=1, source_target_pairs={{0,1},{1,2},{2,3},{4,5},{5,6},{6,7},{8,9},{9,10},{10,11},{12,13},{... | collective-permute-start | bytes 230408 | tf_op jit(solution)/shard_map/ppermute | solution.py:16
  311.3 3.0 multiply_subtract_fusion
  (257 shorter events, 75.7 us)
Async XLA Ops:
  1.9 12.4 %collective-permute-start = (bf16[1,300,128]{2,1,0:T(8,128)(2,1)S(1)}, bf16[1,300,128]{2,1,0:T(8,128)(2,1)S(1)}, u32[]{:S(2)}, u32[]{:S(2)}) collective-permute-start(bf16[1,300,128]{2,1,0:T(8,128)(2,1)S(1)} %bitcast.178), channel_id=1, source_target_pairs={{0,16},{1,17},{2,18},{3,19},{4,20},{5,21},{6,22},{7,23},{8,24},{9,... | collective-permute-start | bytes 230408 | tf_op jit(solution)/shard_map/ppermute | solution.py:16
  6.8 7.6 %collective-permute-start.1 = (bf16[1,300,128]{2,1,0:T(8,128)(2,1)S(1)}, bf16[1,300,128]{2,1,0:T(8,128)(2,1)S(1)}, u32[]{:S(2)}, u32[]{:S(2)}) collective-permute-start(bf16[1,300,128]{2,1,0:T(8,128)(2,1)S(1)} %bitcast.177), channel_id=1, source_target_pairs={{0,4},{4,8},{8,12},{1,5},{5,9},{9,13},{2,6},{6,10},{10,14},{3,7},{... | collective-permute-start | bytes 230408 | tf_op jit(solution)/shard_map/ppermute | solution.py:16
  16.9 12.3 %collective-permute-start.4 = (bf16[1,300,128]{2,1,0:T(8,128)(2,1)S(1)}, bf16[1,300,128]{2,1,0:T(8,128)(2,1)S(1)}, u32[]{:S(2)}, u32[]{:S(2)}) collective-permute-start(bf16[1,300,128]{2,1,0:T(8,128)(2,1)S(1)} %get-tuple-element.52), channel_id=1, source_target_pairs={{16,0},{17,1},{18,2},{19,3},{20,4},{21,5},{22,6},{23,7},{24,8},{25... | collective-permute-start | bytes 230408 | tf_op jit(solution)/shard_map/ppermute | solution.py:17
  18.2 15.6 %collective-permute-start.3 = (bf16[1,300,128]{2,1,0:T(8,128)(2,1)S(1)}, bf16[1,300,128]{2,1,0:T(8,128)(2,1)S(1)}, u32[]{:S(2)}, u32[]{:S(2)}) collective-permute-start(bf16[1,300,128]{2,1,0:T(8,128)(2,1)S(1)} %get-tuple-element.53), channel_id=1, source_target_pairs={{0,16},{1,17},{2,18},{3,19},{4,20},{5,21},{6,22},{7,23},{8,24},{9,... | collective-permute-start | bytes 230408 | tf_op jit(solution)/shard_map/ppermute | solution.py:16
  22.8 11.1 %collective-permute-start.6 = (bf16[1,300,128]{2,1,0:T(8,128)(2,1)S(1)}, bf16[1,300,128]{2,1,0:T(8,128)(2,1)S(1)}, u32[]{:S(2)}, u32[]{:S(2)}) collective-permute-start(bf16[1,300,128]{2,1,0:T(8,128)(2,1)S(1)} %get-tuple-element.50), channel_id=1, source_target_pairs={{4,0},{8,4},{12,8},{5,1},{9,5},{13,9},{6,2},{10,6},{14,10},{7,3},{... | collective-permute-start | bytes 230408 | tf_op jit(solution)/shard_map/ppermute | solution.py:17
  24.1 9.8 %collective-permute-start.5 = (bf16[1,300,128]{2,1,0:T(8,128)(2,1)S(1)}, bf16[1,300,128]{2,1,0:T(8,128)(2,1)S(1)}, u32[]{:S(2)}, u32[]{:S(2)}) collective-permute-start(bf16[1,300,128]{2,1,0:T(8,128)(2,1)S(1)} %get-tuple-element.51), channel_id=1, source_target_pairs={{0,4},{4,8},{8,12},{1,5},{5,9},{9,13},{2,6},{6,10},{10,14},{3,7},{... | collective-permute-start | bytes 230408 | tf_op jit(solution)/shard_map/ppermute | solution.py:16
  88.0 12.2 %collective-permute-start.10 = (bf16[1,300,128]{2,1,0:T(8,128)(2,1)S(1)}, bf16[1,300,128]{2,1,0:T(8,128)(2,1)S(1)}, u32[]{:S(2)}, u32[]{:S(2)}) collective-permute-start(bf16[1,300,128]{2,1,0:T(8,128)(2,1)S(1)} %get-tuple-element.79), channel_id=1, source_target_pairs={{16,0},{17,1},{18,2},{19,3},{20,4},{21,5},{22,6},{23,7},{24,8},{25... | collective-permute-start | bytes 230408 | tf_op jit(solution)/shard_map/ppermute | solution.py:17
  89.3 15.5 %collective-permute-start.9 = (bf16[1,300,128]{2,1,0:T(8,128)(2,1)S(1)}, bf16[1,300,128]{2,1,0:T(8,128)(2,1)S(1)}, u32[]{:S(2)}, u32[]{:S(2)}) collective-permute-start(bf16[1,300,128]{2,1,0:T(8,128)(2,1)S(1)} %get-tuple-element.80), channel_id=1, source_target_pairs={{0,16},{1,17},{2,18},{3,19},{4,20},{5,21},{6,22},{7,23},{8,24},{9,... | collective-permute-start | bytes 230408 | tf_op jit(solution)/shard_map/ppermute | solution.py:16
  93.9 11.0 %collective-permute-start.12 = (bf16[1,300,128]{2,1,0:T(8,128)(2,1)S(1)}, bf16[1,300,128]{2,1,0:T(8,128)(2,1)S(1)}, u32[]{:S(2)}, u32[]{:S(2)}) collective-permute-start(bf16[1,300,128]{2,1,0:T(8,128)(2,1)S(1)} %get-tuple-element.77), channel_id=1, source_target_pairs={{4,0},{8,4},{12,8},{5,1},{9,5},{13,9},{6,2},{10,6},{14,10},{7,3},{... | collective-permute-start | bytes 230408 | tf_op jit(solution)/shard_map/ppermute | solution.py:17
  95.2 9.7 %collective-permute-start.11 = (bf16[1,300,128]{2,1,0:T(8,128)(2,1)S(1)}, bf16[1,300,128]{2,1,0:T(8,128)(2,1)S(1)}, u32[]{:S(2)}, u32[]{:S(2)}) collective-permute-start(bf16[1,300,128]{2,1,0:T(8,128)(2,1)S(1)} %get-tuple-element.78), channel_id=1, source_target_pairs={{0,4},{4,8},{8,12},{1,5},{5,9},{9,13},{2,6},{6,10},{10,14},{3,7},{... | collective-permute-start | bytes 230408 | tf_op jit(solution)/shard_map/ppermute | solution.py:16
  109.9 11.5 %collective-permute-start.16 = (bf16[1,300,128]{2,1,0:T(8,128)(2,1)S(1)}, bf16[1,300,128]{2,1,0:T(8,128)(2,1)S(1)}, u32[]{:S(2)}, u32[]{:S(2)}) collective-permute-start(bf16[1,300,128]{2,1,0:T(8,128)(2,1)S(1)} %get-tuple-element.43), channel_id=1, source_target_pairs={{16,0},{17,1},{18,2},{19,3},{20,4},{21,5},{22,6},{23,7},{24,8},{25... | collective-permute-start | bytes 230408 | tf_op jit(solution)/shard_map/ppermute | solution.py:17
  111.2 15.5 %collective-permute-start.15 = (bf16[1,300,128]{2,1,0:T(8,128)(2,1)S(1)}, bf16[1,300,128]{2,1,0:T(8,128)(2,1)S(1)}, u32[]{:S(2)}, u32[]{:S(2)}) collective-permute-start(bf16[1,300,128]{2,1,0:T(8,128)(2,1)S(1)} %get-tuple-element.44), channel_id=1, source_target_pairs={{0,16},{1,17},{2,18},{3,19},{4,20},{5,21},{6,22},{7,23},{8,24},{9,... | collective-permute-start | bytes 230408 | tf_op jit(solution)/shard_map/ppermute | solution.py:16
  115.8 11.0 %collective-permute-start.18 = (bf16[1,300,128]{2,1,0:T(8,128)(2,1)S(1)}, bf16[1,300,128]{2,1,0:T(8,128)(2,1)S(1)}, u32[]{:S(2)}, u32[]{:S(2)}) collective-permute-start(bf16[1,300,128]{2,1,0:T(8,128)(2,1)S(1)} %get-tuple-element.41), channel_id=1, source_target_pairs={{4,0},{8,4},{12,8},{5,1},{9,5},{13,9},{6,2},{10,6},{14,10},{7,3},{... | collective-permute-start | bytes 230408 | tf_op jit(solution)/shard_map/ppermute | solution.py:17
  117.1 9.7 %collective-permute-start.17 = (bf16[1,300,128]{2,1,0:T(8,128)(2,1)S(1)}, bf16[1,300,128]{2,1,0:T(8,128)(2,1)S(1)}, u32[]{:S(2)}, u32[]{:S(2)}) collective-permute-start(bf16[1,300,128]{2,1,0:T(8,128)(2,1)S(1)} %get-tuple-element.42), channel_id=1, source_target_pairs={{0,4},{4,8},{8,12},{1,5},{5,9},{9,13},{2,6},{6,10},{10,14},{3,7},{... | collective-permute-start | bytes 230408 | tf_op jit(solution)/shard_map/ppermute | solution.py:16
  184.7 14.7 %collective-permute-start.22 = (bf16[1,300,128]{2,1,0:T(8,128)(2,1)}, bf16[1,300,128]{2,1,0:T(8,128)(2,1)}, u32[]{:S(2)}, u32[]{:S(2)}) collective-permute-start(bf16[1,300,128]{2,1,0:T(8,128)(2,1)} %get-tuple-element.70), channel_id=1, source_target_pairs={{16,0},{17,1},{18,2},{19,3},{20,4},{21,5},{22,6},{23,7},{24,8},{25... | collective-permute-start | bytes 230408 | tf_op jit(solution)/shard_map/ppermute | solution.py:17
  186.0 18.0 %collective-permute-start.21 = (bf16[1,300,128]{2,1,0:T(8,128)(2,1)S(1)}, bf16[1,300,128]{2,1,0:T(8,128)(2,1)}, u32[]{:S(2)}, u32[]{:S(2)}) collective-permute-start(bf16[1,300,128]{2,1,0:T(8,128)(2,1)S(1)} %get-tuple-element.71), channel_id=1, source_target_pairs={{0,16},{1,17},{2,18},{3,19},{4,20},{5,21},{6,22},{7,23},{8,24},{9,... | collective-permute-start | bytes 230408 | tf_op jit(solution)/shard_map/ppermute | solution.py:16
  191.8 13.2 %collective-permute-start.24 = (bf16[1,300,128]{2,1,0:T(8,128)(2,1)S(1)}, bf16[1,300,128]{2,1,0:T(8,128)(2,1)}, u32[]{:S(2)}, u32[]{:S(2)}) collective-permute-start(bf16[1,300,128]{2,1,0:T(8,128)(2,1)S(1)} %get-tuple-element.68), channel_id=1, source_target_pairs={{4,0},{8,4},{12,8},{5,1},{9,5},{13,9},{6,2},{10,6},{14,10},{7,3},{... | collective-permute-start | bytes 230408 | tf_op jit(solution)/shard_map/ppermute | solution.py:17
  193.1 12.0 %collective-permute-start.23 = (bf16[1,300,128]{2,1,0:T(8,128)(2,1)S(1)}, bf16[1,300,128]{2,1,0:T(8,128)(2,1)}, u32[]{:S(2)}, u32[]{:S(2)}) collective-permute-start(bf16[1,300,128]{2,1,0:T(8,128)(2,1)S(1)} %get-tuple-element.69), channel_id=1, source_target_pairs={{0,4},{4,8},{8,12},{1,5},{5,9},{9,13},{2,6},{6,10},{10,14},{3,7},{... | collective-permute-start | bytes 230408 | tf_op jit(solution)/shard_map/ppermute | solution.py:16
  196.8 9.3 %collective-permute-start.26 = (bf16[1,300,128]{2,1,0:T(8,128)(2,1)S(1)}, bf16[1,300,128]{2,1,0:T(8,128)(2,1)S(1)}, u32[]{:S(2)}, u32[]{:S(2)}) collective-permute-start(bf16[1,300,128]{2,1,0:T(8,128)(2,1)S(1)} %get-tuple-element.67), channel_id=1, source_target_pairs={{1,0},{2,1},{3,2},{5,4},{6,5},{7,6},{9,8},{10,9},{11,10},{13,12},{... | collective-permute-start | bytes 230408 | tf_op jit(solution)/shard_map/ppermute | solution.py:17
  199.5 7.2 %collective-permute-start.25 = (bf16[1,300,128]{2,1,0:T(8,128)(2,1)S(1)}, bf16[1,300,128]{2,1,0:T(8,128)(2,1)S(1)}, u32[]{:S(2)}, u32[]{:S(2)}) collective-permute-start(bf16[1,300,128]{2,1,0:T(8,128)(2,1)S(1)} %get-tuple-element.66), channel_id=1, source_target_pairs={{0,1},{1,2},{2,3},{4,5},{5,6},{6,7},{8,9},{9,10},{10,11},{12,13},{... | collective-permute-start | bytes 230408 | tf_op jit(solution)/shard_map/ppermute | solution.py:16
  209.9 11.5 %collective-permute-start.28 = (bf16[1,300,128]{2,1,0:T(8,128)(2,1)S(1)}, bf16[1,300,128]{2,1,0:T(8,128)(2,1)S(1)}, u32[]{:S(2)}, u32[]{:S(2)}) collective-permute-start(bf16[1,300,128]{2,1,0:T(8,128)(2,1)S(1)} %get-tuple-element.34), channel_id=1, source_target_pairs={{16,0},{17,1},{18,2},{19,3},{20,4},{21,5},{22,6},{23,7},{24,8},{25... | collective-permute-start | bytes 230408 | tf_op jit(solution)/shard_map/ppermute | solution.py:17
  211.2 15.3 %collective-permute-start.27 = (bf16[1,300,128]{2,1,0:T(8,128)(2,1)S(1)}, bf16[1,300,128]{2,1,0:T(8,128)(2,1)S(1)}, u32[]{:S(2)}, u32[]{:S(2)}) collective-permute-start(bf16[1,300,128]{2,1,0:T(8,128)(2,1)S(1)} %get-tuple-element.35), channel_id=1, source_target_pairs={{0,16},{1,17},{2,18},{3,19},{4,20},{5,21},{6,22},{7,23},{8,24},{9,... | collective-permute-start | bytes 230408 | tf_op jit(solution)/shard_map/ppermute | solution.py:16
  215.8 10.8 %collective-permute-start.30 = (bf16[1,300,128]{2,1,0:T(8,128)(2,1)S(1)}, bf16[1,300,128]{2,1,0:T(8,128)(2,1)S(1)}, u32[]{:S(2)}, u32[]{:S(2)}) collective-permute-start(bf16[1,300,128]{2,1,0:T(8,128)(2,1)S(1)} %get-tuple-element.32), channel_id=1, source_target_pairs={{4,0},{8,4},{12,8},{5,1},{9,5},{13,9},{6,2},{10,6},{14,10},{7,3},{... | collective-permute-start | bytes 230408 | tf_op jit(solution)/shard_map/ppermute | solution.py:17
  217.1 9.5 %collective-permute-start.29 = (bf16[1,300,128]{2,1,0:T(8,128)(2,1)S(1)}, bf16[1,300,128]{2,1,0:T(8,128)(2,1)S(1)}, u32[]{:S(2)}, u32[]{:S(2)}) collective-permute-start(bf16[1,300,128]{2,1,0:T(8,128)(2,1)S(1)} %get-tuple-element.33), channel_id=1, source_target_pairs={{0,4},{4,8},{8,12},{1,5},{5,9},{9,13},{2,6},{6,10},{10,14},{3,7},{... | collective-permute-start | bytes 230408 | tf_op jit(solution)/shard_map/ppermute | solution.py:16
  220.1 7.1 %collective-permute-start.32 = (bf16[1,300,128]{2,1,0:T(8,128)(2,1)S(1)}, bf16[1,300,128]{2,1,0:T(8,128)(2,1)S(1)}, u32[]{:S(2)}, u32[]{:S(2)}) collective-permute-start(bf16[1,300,128]{2,1,0:T(8,128)(2,1)S(1)} %get-tuple-element.31), channel_id=1, source_target_pairs={{1,0},{2,1},{3,2},{5,4},{6,5},{7,6},{9,8},{10,9},{11,10},{13,12},{... | collective-permute-start | bytes 230408 | tf_op jit(solution)/shard_map/ppermute | solution.py:17
  221.4 7.6 %collective-permute-start.31 = (bf16[1,300,128]{2,1,0:T(8,128)(2,1)S(1)}, bf16[1,300,128]{2,1,0:T(8,128)(2,1)S(1)}, u32[]{:S(2)}, u32[]{:S(2)}) collective-permute-start(bf16[1,300,128]{2,1,0:T(8,128)(2,1)S(1)} %get-tuple-element.30), channel_id=1, source_target_pairs={{0,1},{1,2},{2,3},{4,5},{5,6},{6,7},{8,9},{9,10},{10,11},{12,13},{... | collective-permute-start | bytes 230408 | tf_op jit(solution)/shard_map/ppermute | solution.py:16
  285.7 17.3 %collective-permute-start.34 = (bf16[1,300,128]{2,1,0:T(8,128)(2,1)}, bf16[1,300,128]{2,1,0:T(8,128)(2,1)}, u32[]{:S(2)}, u32[]{:S(2)}) collective-permute-start(bf16[1,300,128]{2,1,0:T(8,128)(2,1)} %get-tuple-element.61), channel_id=1, source_target_pairs={{16,0},{17,1},{18,2},{19,3},{20,4},{21,5},{22,6},{23,7},{24,8},{25... | collective-permute-start | bytes 230408 | tf_op jit(solution)/shard_map/ppermute | solution.py:17
  287.0 20.6 %collective-permute-start.33 = (bf16[1,300,128]{2,1,0:T(8,128)(2,1)}, bf16[1,300,128]{2,1,0:T(8,128)(2,1)}, u32[]{:S(2)}, u32[]{:S(2)}) collective-permute-start(bf16[1,300,128]{2,1,0:T(8,128)(2,1)} %get-tuple-element.62), channel_id=1, source_target_pairs={{0,16},{1,17},{2,18},{3,19},{4,20},{5,21},{6,22},{7,23},{8,24},{9,... | collective-permute-start | bytes 230408 | tf_op jit(solution)/shard_map/ppermute | solution.py:16
  292.8 15.9 %collective-permute-start.36 = (bf16[1,300,128]{2,1,0:T(8,128)(2,1)}, bf16[1,300,128]{2,1,0:T(8,128)(2,1)}, u32[]{:S(2)}, u32[]{:S(2)}) collective-permute-start(bf16[1,300,128]{2,1,0:T(8,128)(2,1)} %get-tuple-element.59), channel_id=1, source_target_pairs={{4,0},{8,4},{12,8},{5,1},{9,5},{13,9},{6,2},{10,6},{14,10},{7,3},{... | collective-permute-start | bytes 230408 | tf_op jit(solution)/shard_map/ppermute | solution.py:17
  294.1 14.6 %collective-permute-start.35 = (bf16[1,300,128]{2,1,0:T(8,128)(2,1)}, bf16[1,300,128]{2,1,0:T(8,128)(2,1)}, u32[]{:S(2)}, u32[]{:S(2)}) collective-permute-start(bf16[1,300,128]{2,1,0:T(8,128)(2,1)} %get-tuple-element.60), channel_id=1, source_target_pairs={{0,4},{4,8},{8,12},{1,5},{5,9},{9,13},{2,6},{6,10},{10,14},{3,7},{... | collective-permute-start | bytes 230408 | tf_op jit(solution)/shard_map/ppermute | solution.py:16
  297.8 12.1 %collective-permute-start.38 = (bf16[1,300,128]{2,1,0:T(8,128)(2,1)}, bf16[1,300,128]{2,1,0:T(8,128)(2,1)}, u32[]{:S(2)}, u32[]{:S(2)}) collective-permute-start(bf16[1,300,128]{2,1,0:T(8,128)(2,1)} %get-tuple-element.58), channel_id=1, source_target_pairs={{1,0},{2,1},{3,2},{5,4},{6,5},{7,6},{9,8},{10,9},{11,10},{13,12},{... | collective-permute-start | bytes 230408 | tf_op jit(solution)/shard_map/ppermute | solution.py:17
  303.0 7.2 %collective-permute-start.37 = (bf16[1,300,128]{2,1,0:T(8,128)(2,1)S(1)}, bf16[1,300,128]{2,1,0:T(8,128)(2,1)S(1)}, u32[]{:S(2)}, u32[]{:S(2)}) collective-permute-start(bf16[1,300,128]{2,1,0:T(8,128)(2,1)S(1)} %get-tuple-element.57), channel_id=1, source_target_pairs={{0,1},{1,2},{2,3},{4,5},{5,6},{6,7},{8,9},{9,10},{10,11},{12,13},{... | collective-permute-start | bytes 230408 | tf_op jit(solution)/shard_map/ppermute | solution.py:16
  (40 other events, 871.5 us)
where the time goes:
time: 319 us; the launch traced here: 317 us
  blocking collectives  123 us (39%)
  starting transfers between devices  111 us (35%)
  matrix products  26 us (8%)
  other arithmetic  23.1 us (7%)
  local copies, waits for them, and re-layouts  22.2 us (7%)
  waiting for transfers between devices  8.58 us (3%)
    psum x3, blocking collectives, merged_operator(): lax.psum((coarse_part, owned_inner(current, precond_res), energy_local),...  123 us
    ppermute x21, starting transfers between devices, with_halo(): before = lax.ppermute(last, axis, up)  88.2 us
    ppermute x18, starting transfers between devices, with_halo(): after = lax.ppermute(first, axis, down)  23.2 us
    dot_general x3, matrix products, local_terms(): local_image = jnp.dot(flex, signed, preferred_element_type=jnp.float32)  16 us
    ppermute x21, waiting for transfers between devices, with_halo(): before = lax.ppermute(last, axis, up)  7.79 us
  transfers between devices with their start and end apart: 39, of which 8 were waited for; matrix products, arithmetic and copies ran while one was open for 4% of the time, Pallas kernels for 0%

commit v1 on v0

v1 whole, which is shorter than its diff:
```python
import functools

import jax
import jax.numpy as jnp
from jax import lax
from jax.experimental import pallas as pl
from jax.experimental.pallas import tpu as pltpu
from jax.sharding import PartitionSpec as P

ITERS = 3
AXES = ("gx", "gy", "gz")
F32 = jnp.float32
BF16 = jnp.bfloat16
MESH = pl.DeviceIdType.MESH


def round_up(value, unit):
    return (value + unit - 1) // unit * unit


def kernel(
    sizes,
    dims,
    rhs_hbm,
    flex_hbm,
    coup_hbm,
    stiff_hbm,
    cinv_hbm,
    ids_ref,
    mult_ref,
    resid_ref,
    rhs_v,
    flex_v,
    coup_v,
    k_own,
    k_nb,
    cinv_v,
    r_send,
    r_recv,
    casm_wide,
    casm_v,
    c_own,
    c_nb,
    corr_v,
    res_v,
    z_v,
    zflat,
    signed_v,
    imgflat,
    img_send,
    img_recv,
    dir_v,
    s_v,
    lam_v,
    coarse_a,
    coarse_b,
    energy_a,
    energy_b,
    local_sem,
    setup_send,
    setup_recv,
    halo_send,
    halo_recv,
    a_send,
    a_recv,
    b_send,
    b_recv,
    ea_send,
    ea_recv,
    eb_send,
    eb_recv,
):
    nx, ny, nz = sizes
    faces, width, cols, ncoarse, corners = dims
    total = faces * width
    ncq = c_own.shape[1]
    wide = c_own.shape[2]
    prow = coarse_a.shape[2]
    here = [lax.axis_index(name) for name in AXES]
    plane = nx * ny
    me_plane = here[0] * ny + here[1]
    has = []
    for axis in range(3):
        has.append(here[axis] > 0)
        has.append(here[axis] < sizes[axis] - 1)
    masks = [jnp.where(flag, 1.0, 0.0).astype(F32) for flag in has]

    def neighbour(face):
        axis = face // 2
        step = 1 if face % 2 else -1
        spot = jnp.clip(here[axis] + step, 0, sizes[axis] - 1)
        return {AXES[axis]: spot}

    def plane_peer(offset):
        index = lax.rem(me_plane + offset, plane)
        return {"gx": index // ny, "gy": lax.rem(index, ny)}

    def z_peer(offset):
        return {"gz": lax.rem(here[2] + offset, nz)}

    loads = []
    for index, (src, dst) in enumerate(
        ((rhs_hbm, rhs_v), (coup_hbm, coup_v), (cinv_hbm, cinv_v), (stiff_hbm, k_own), (flex_hbm, flex_v))
    ):
        copy = pltpu.make_async_copy(src, dst, local_sem.at[index])
        copy.start()
        loads.append(copy)

    for face in range(faces):

        @pl.when(jnp.logical_not(has[face]))
        def _(face=face):
            k_nb[face] = jnp.zeros(k_nb.shape[1:], BF16)
            c_nb[face] = jnp.zeros(c_nb.shape[1:], BF16)
            for it in range(ITERS):
                img_recv[it, face] = jnp.zeros((width, cols), BF16)

    for axis in range(3):

        @pl.when(jnp.logical_not(has[2 * axis]))
        def _(axis=axis):
            r_recv[axis] = jnp.zeros((width, cols), BF16)

    barrier = pltpu.get_barrier_semaphore()
    for offset in range(1, plane):
        pl.semaphore_signal(barrier, inc=1, device_id=plane_peer(offset), device_id_type=MESH)
    for offset in range(1, nz):
        pl.semaphore_signal(barrier, inc=1, device_id=z_peer(offset), device_id_type=MESH)

    loads[0].wait()
    for axis in range(3):
        r_send[axis] = (rhs_v[axis] * masks[2 * axis + 1]).astype(BF16)
    pl.semaphore_wait(barrier, plane - 1 + nz - 1)

    def remote(src, dst, send_sem, recv_sem, target):
        return pltpu.make_async_remote_copy(
            src_ref=src, dst_ref=dst, send_sem=send_sem, recv_sem=recv_sem, device_id=target, device_id_type=MESH
        )

    def rhs_copy(axis):
        return remote(
            r_send.at[axis], r_recv.at[axis], setup_send.at[0, 2 * axis + 1], setup_recv.at[0, 2 * axis],
            neighbour(2 * axis + 1),
        )

    def k_copy(face):
        return remote(
            stiff_hbm.at[face], k_nb.at[face ^ 1], setup_send.at[1, face], setup_recv.at[1, face ^ 1], neighbour(face)
        )

    def c_copy(face):
        return remote(
            c_own.at[face], c_nb.at[face ^ 1], setup_send.at[2, face], setup_recv.at[2, face ^ 1], neighbour(face)
        )

    def halo_copy(it, face):
        return remote(
            img_send.at[it, face], img_recv.at[it, face ^ 1], halo_send.at[it, face], halo_recv.at[it, face ^ 1],
            neighbour(face),
        )

    def when_has(face, action):
        @pl.when(has[face])
        def _():
            action()

    for axis in (2, 0, 1):
        when_has(2 * axis + 1, lambda axis=axis: rhs_copy(axis).start())
    for face in (4, 0, 2, 5, 1, 3):
        when_has(face, lambda face=face: k_copy(face).start())

    loads[1].wait()
    lane = lax.broadcasted_iota(jnp.int32, (1, 3 * corners), 1)
    target_row = jnp.full((1, 3 * corners), -1, jnp.int32)
    for k in range(corners):
        node = ids_ref[k]
        mine = (lane >= 3 * k) & (lane < 3 * k + 3) & (node >= 0)
        target_row = jnp.where(mine, 3 * node + lane - 3 * k, target_row)
    rows = lax.broadcasted_iota(jnp.int32, (ncq, 3 * corners), 0)
    assembly = jnp.where(rows == target_row, 1.0, 0.0).astype(BF16)
    assembled = jnp.dot(assembly, coup_v[...], preferred_element_type=F32)
    casm_v[...] = assembled.astype(BF16)
    casm_wide[...] = jnp.zeros(casm_wide.shape, F32)
    casm_wide[:, 0:total] = assembled
    span = casm_wide.shape[1]
    lanes = lax.broadcasted_iota(jnp.int32, (ncq, wide), 1)
    for face in range(faces):
        start = face * width
        low = start // 128 * 128
        high = min(round_up(start + width, 128), span)
        piece = casm_wide[:, low:high]
        if start > low:
            piece = pltpu.roll(piece, (high - low) - (start - low), 1)
        piece = piece[:, 0:wide]
        c_own[face] = jnp.where(lanes < width, piece, 0.0).astype(BF16)
        when_has(face, lambda face=face: c_copy(face).start())

    for axis in range(3):
        when_has(2 * axis, lambda axis=axis: rhs_copy(axis).wait_recv())
        res_v[2 * axis] = -r_recv[axis].astype(F32)
        res_v[2 * axis + 1] = rhs_v[axis] * masks[2 * axis + 1]
    loads[2].wait()
    loads[3].wait()

    coarse_row = lax.broadcasted_iota(jnp.int32, (prow, cols), 0)
    rho_now = None
    step_size = None
    for it in range(ITERS):
        last = it + 1 == ITERS
        rho_acc = jnp.zeros((1, cols), F32)
        for face in range(faces):
            if it == 0:
                when_has(face, lambda face=face: k_copy(face).wait_send())
                when_has(face, lambda face=face: remote(
                    stiff_hbm.at[face], k_nb.at[face], setup_send.at[1, face], setup_recv.at[1, face], neighbour(face)
                ).wait_recv())
            res = res_v[face]
            half = (0.5 * res).astype(BF16)
            z = jnp.dot(k_own[face], half, preferred_element_type=F32)
            z = z + jnp.dot(k_nb[face], half, preferred_element_type=F32)
            z = z * (0.5 * masks[face])
            z_v[face] = z
            zflat[face * width : (face + 1) * width, :] = z
            if face % 2:
                rho_acc = rho_acc + jnp.sum(res * z, axis=0, keepdims=True)
        signed = zflat[...].astype(BF16)
        signed_v[...] = signed
        if it == 0:
            loads[4].wait()
        coarse_part = jnp.dot(casm_v[...], signed, preferred_element_type=F32)
        if prow > ncq:
            coarse_part = jnp.concatenate([coarse_part, jnp.zeros((prow - ncq, cols), F32)], axis=0)
        coarse_a[it, 0] = jnp.where(coarse_row == ncoarse, rho_acc, coarse_part[0:prow])

        def a_copy(offset, it=it):
            return remote(
                coarse_a.at[it, 0], coarse_a.at[it, offset], a_send.at[it, offset], a_recv.at[it, offset],
                plane_peer(offset),
            )

        def b_copy(offset, it=it):
            return remote(
                coarse_b.at[it, 0], coarse_b.at[it, offset], b_send.at[it, offset], b_recv.at[it, offset],
                z_peer(offset),
            )

        def ea_copy(offset, it=it):
            return remote(
                energy_a.at[it, 0], energy_a.at[it, offset], ea_send.at[it, offset], ea_recv.at[it, offset],
                plane_peer(offset),
            )

        def eb_copy(offset, it=it):
            return remote(
                energy_b.at[it, 0], energy_b.at[it, offset], eb_send.at[it, offset], eb_recv.at[it, offset],
                z_peer(offset),
            )

        for offset in range(1, plane):
            a_copy(offset).start()

        energy_acc = jnp.zeros((8, cols), F32)
        begin = 0
        for face in range(faces):
            end = total if face + 1 == faces else round_up((face + 1) * width, 16)
            image = jnp.dot(flex_v[begin:end, :], signed_v[...], preferred_element_type=F32)
            imgflat[begin:end, :] = image
            weighted = image * signed_v[begin:end, :].astype(F32)
            energy_acc = energy_acc + jnp.sum(weighted.reshape(-1, 8, cols), axis=0)
            begin = end
            img_send[it, face] = imgflat[face * width : (face + 1) * width, :].astype(BF16)
            if not last or face % 2 == 0:
                when_has(face, lambda face=face, it=it: halo_copy(it, face).start())
        energy_a[it, 0] = energy_acc
        for offset in range(1, plane):
            ea_copy(offset).start()

        part = coarse_a[it, 0]
        for offset in range(1, plane):
            a_copy(offset).wait_recv()
            part = part + coarse_a[it, offset]
        coarse_b[it, 0] = part
        for offset in range(1, nz):
            b_copy(offset).start()
        energy = energy_a[it, 0]
        for offset in range(1, plane):
            ea_copy(offset).wait_recv()
            energy = energy + energy_a[it, offset]
        energy_b[it, 0] = energy
        for offset in range(1, nz):
            eb_copy(offset).start()

        if it == 0:
            for face in range(faces):
                when_has(face, lambda face=face: remote(
                    c_own.at[face], c_nb.at[face], setup_send.at[2, face], setup_recv.at[2, face], neighbour(face)
                ).wait_recv())
                own = c_own[face].astype(F32)
                other = c_nb[face].astype(F32)
                stack = jnp.concatenate([own, -other] * (corr_v.shape[2] // (2 * ncq)), axis=0)
                corr_v[face] = stack.T[0:width].astype(BF16)

        coarse = coarse_b[it, 0]
        for offset in range(1, nz):
            b_copy(offset).wait_recv()
            coarse = coarse + coarse_b[it, offset]
        rho = jnp.sum(jnp.where(coarse_row == ncoarse, coarse, 0.0), axis=0, keepdims=True)
        if prow > ncq:
            coarse = coarse[0:ncq]
        elif prow < ncq:
            coarse = jnp.concatenate([coarse, jnp.zeros((ncq - prow, cols), F32)], axis=0)
        rows_q = lax.broadcasted_iota(jnp.int32, (ncq, cols), 0)
        coarse = jnp.where(rows_q < ncoarse, coarse, 0.0)
        sol = jnp.dot(cinv_v[...], coarse[0:ncoarse].astype(BF16), preferred_element_type=F32)
        sol = jnp.concatenate([sol, jnp.zeros((ncq - ncoarse, cols), F32)], axis=0) if ncq > ncoarse else sol
        sol_hi = sol.astype(BF16)
        sol_lo = (sol - sol_hi.astype(F32)).astype(BF16)
        if corr_v.shape[2] == 4 * ncq:
            sol_parts = [jnp.concatenate([sol_hi, sol_hi, sol_lo, sol_lo], axis=0)]
        else:
            sol_parts = [jnp.concatenate([piece, piece], axis=0) for piece in (sol_hi, sol_lo)]
        coarse_energy = jnp.sum(coarse * sol, axis=0, keepdims=True)

        energy = energy_b[it, 0]
        for offset in range(1, nz):
            eb_copy(offset).wait_recv()
            energy = energy + energy_b[it, offset]
        energy = jnp.sum(energy, axis=0, keepdims=True) + coarse_energy

        if it == 0:
            step_size = rho / energy
            beta = None
        else:
            beta = rho / rho_now
            step_size = rho / (energy - beta * rho / step_size)
        rho_now = rho

        for face in range(faces):
            if last and face % 2 == 0:
                continue
            when_has(face, lambda face=face, it=it: remote(
                img_send.at[it, face], img_recv.at[it, face], halo_send.at[it, face], halo_recv.at[it, face],
                neighbour(face),
            ).wait_recv())
            image = img_send[it, face].astype(F32) - img_recv[it, face].astype(F32)
            for piece in sol_parts:
                image = image + jnp.dot(corr_v[face], piece, preferred_element_type=F32)
            image = image * masks[face]
            if it > 0:
                image = image + beta * s_v[face]
            new_res = res_v[face] - step_size * image
            if last:
                resid_ref[face // 2] = new_res
            else:
                s_v[face] = image
                res_v[face] = new_res
            if face % 2:
                axis = face // 2
                direction = z_v[face]
                if it > 0:
                    direction = direction + beta * dir_v[axis]
                if not last:
                    dir_v[axis] = direction
                moved = step_size * direction
                if it > 0:
                    moved = moved + lam_v[axis]
                if last:
                    mult_ref[axis] = moved
                else:
                    lam_v[axis] = moved

    for axis in range(3):
        when_has(2 * axis + 1, lambda axis=axis: rhs_copy(axis).wait_send())
    for face in range(faces):
        when_has(face, lambda face=face: c_copy(face).wait_send())
        for it in range(ITERS):
            if it + 1 < ITERS or face % 2 == 0:
                when_has(face, lambda face=face, it=it: halo_copy(it, face).wait_send())
    for it in range(ITERS):
        for offset in range(1, plane):
            remote(coarse_a.at[it, 0], coarse_a.at[it, offset], a_send.at[it, offset], a_recv.at[it, offset],
                   plane_peer(offset)).wait_send()
            remote(energy_a.at[it, 0], energy_a.at[it, offset], ea_send.at[it, offset], ea_recv.at[it, offset],
                   plane_peer(offset)).wait_send()
        for offset in range(1, nz):
            remote(coarse_b.at[it, 0], coarse_b.at[it, offset], b_send.at[it, offset], b_recv.at[it, offset],
                   z_peer(offset)).wait_send()
            remote(energy_b.at[it, 0], energy_b.at[it, offset], eb_send.at[it, offset], eb_recv.at[it, offset],
                   z_peer(offset)).wait_send()


def body(sizes, dual_rhs, local_flex, corner_coupling, face_stiffness, coarse_inverse, corner_ids):
    rhs = dual_rhs[0, 0, 0]
    flex = local_flex[0, 0, 0]
    coupling = corner_coupling[0, 0, 0]
    stiffness = face_stiffness[0, 0, 0]
    ids = corner_ids[0, 0, 0]
    faces, width, _ = stiffness.shape
    cols = rhs.shape[2]
    ncoarse = coarse_inverse.shape[0]
    corners = ids.shape[0]
    total = faces * width
    ncq = round_up(ncoarse, 32)
    prow = round_up(ncoarse + 1, 8)
    wide = round_up(width, 128)
    span = round_up((faces - 1) * width // 128 * 128 + max(round_up(width + 127, 128), wide), 128)
    nx, ny, nz = sizes
    plane = nx * ny
    dma = pltpu.SemaphoreType.DMA
    any_space = pl.BlockSpec(memory_space=pl.ANY)
    vmem = pl.BlockSpec(memory_space=pltpu.VMEM)
    smem = pl.BlockSpec(memory_space=pltpu.SMEM)
    out = jax.ShapeDtypeStruct(rhs.shape, F32)
    mult, resid = pl.pallas_call(
        functools.partial(kernel, sizes, (faces, width, cols, ncoarse, corners)),
        out_shape=(out, out),
        in_specs=[any_space] * 5 + [smem],
        out_specs=(vmem, vmem),
        scratch_shapes=[
            pltpu.VMEM(rhs.shape, F32),
            pltpu.VMEM(flex.shape, BF16),
            pltpu.VMEM(coupling.shape, BF16),
            pltpu.VMEM(stiffness.shape, BF16),
            pltpu.VMEM(stiffness.shape, BF16),
            pltpu.VMEM(coarse_inverse.shape, BF16),
            pltpu.VMEM((3, width, cols), BF16),
            pltpu.VMEM((3, width, cols), BF16),
            pltpu.VMEM((ncq, span), F32),
            pltpu.VMEM((ncq, total), BF16),
            pltpu.VMEM((faces, ncq, wide), BF16),
            pltpu.VMEM((faces, ncq, wide), BF16),
            pltpu.VMEM((faces, width, (4 if ncq <= 64 else 2) * ncq), BF16),
            pltpu.VMEM((faces, width, cols), F32),
            pltpu.VMEM((faces, width, cols), F32),
            pltpu.VMEM((total, cols), F32),
            pltpu.VMEM((total, cols), BF16),
            pltpu.VMEM((total, cols), F32),
            pltpu.VMEM((ITERS, faces, width, cols), BF16),
            pltpu.VMEM((ITERS, faces, width, cols), BF16),
            pltpu.VMEM((3, width, cols), F32),
            pltpu.VMEM((faces, width, cols), F32),
            pltpu.VMEM((3, width, cols), F32),
            pltpu.VMEM((ITERS, plane, prow, cols), F32),
            pltpu.VMEM((ITERS, nz, prow, cols), F32),
            pltpu.VMEM((ITERS, plane, 8, cols), F32),
            pltpu.VMEM((ITERS, nz, 8, cols), F32),
            dma((5,)),
            dma((3, faces)),
            dma((3, faces)),
            dma((ITERS, faces)),
            dma((ITERS, faces)),
            dma((ITERS, plane)),
            dma((ITERS, plane)),
            dma((ITERS, nz)),
            dma((ITERS, nz)),
            dma((ITERS, plane)),
            dma((ITERS, plane)),
            dma((ITERS, nz)),
            dma((ITERS, nz)),
        ],
        compiler_params=pltpu.CompilerParams(
            collective_id=0, has_side_effects=True, vmem_limit_bytes=62 * 1024 * 1024
        ),
    )(rhs, flex, coupling, stiffness, coarse_inverse, ids)
    return (mult[None, None, None], resid[None, None, None])


def solution(mesh):
    sizes = tuple(mesh.shape[name] for name in AXES)
    placed = (
        P("gx", "gy", "gz", None, None, None),
        P("gx", "gy", "gz", None, None),
        P("gx", "gy", "gz", None, None),
        P("gx", "gy", "gz", None, None, None),
        P(),
        P("gx", "gy", "gz", None),
    )
    return jax.shard_map(
        functools.partial(body, sizes),
        mesh=mesh,
        in_specs=placed,
        out_specs=(P("gx", "gy", "gz", None, None, None), P("gx", "gy", "gz", None, None, None)),
        check_vma=False,
    )
```

time: 319 us -> 67.4 us (0.21)
  blocking collectives: 123 us -> 0 us
  starting transfers between devices: 111 us -> 0 us
  Pallas kernels: 0 us -> 60.2 us
  matrix products: 26 us -> 0 us
  other arithmetic: 23.1 us -> 0 us
  local copies, waits for them, and re-layouts: 22.2 us -> 6.35 us
  waiting for transfers between devices: 8.58 us -> 0 us
    psum x3 -> x0, blocking collectives: 123 us -> none  [merged_operator(): lax.psum((coarse_part, owned_inner(current, precond_res), energy_local),...]
    ppermute x39 -> x0, starting transfers between devices: 111 us -> none  [the longest x21 88.2 us: with_halo(): before = lax.ppermute(last, axis, up)]
    pallas_call x0 -> x1, Pallas kernels: none -> 60.2 us  [body(): pl.pallas_call(functools.partial(kernel, sizes, (faces, width, cols, ncoa...]
    dot_general x21 -> x0, matrix products: 26 us -> none  [the longest x3 16 us: local_terms(): local_image = jnp.dot(flex, signed, preferred_element_type=jnp.float32)]
    ppermute x39 -> x0, waiting for transfers between devices: 8.58 us -> none  [the longest x21 7.79 us: with_halo(): before = lax.ppermute(last, axis, up)]
    convert_element_type x21 -> x0, other arithmetic: 8.47 us -> none  [the longest x2 2.79 us: local_terms(): (face_sign * direction).astype(jnp.bfloat16)]
    convert_element_type x12 -> x0, local copies, waits for them, and re-layouts: 8.06 us -> none  [the longest x3 4.6 us: local_terms(): (face_sign * direction).astype(jnp.bfloat16)]
    sub x3 -> x0, other arithmetic: 5.93 us -> none  [body(): residual = residual - step_size * direction_image]
  transfers between devices with their start and end apart: 39 -> 0, of which waited for: 8 -> 0; matrix products, arithmetic and copies ran while one was open for 4% -> 0% of each run, Pallas kernels for 0% -> 0%
where the time goes in v1:
time: 67.4 us; the launch traced here: 67.2 us
  Pallas kernels  60.2 us (89%)
  local copies, waits for them, and re-layouts  6.35 us (9%)
    pallas_call x1, Pallas kernels, body(): pl.pallas_call(functools.partial(kernel, sizes, (faces, width, cols, ncoa...  60.2 us
    unnamed x3, local copies, waits for them, and re-layouts  6.35 us

profile of v1, /device:TPU:0, one launch (start us, length us, event | category | flops | bytes accessed | tf_op | source)
XLA Modules:
  0.0 67.2 jit_solution(6706704613463315298)
XLA Ops:
  0.6 1.8 %copy.12 = f32[1,1,1,3,300,128]{5,4,2,3,1,0:T(8,128)} copy(f32[1,1,1,3,300,128]{5,2,4,3,1,0:T(1,128)} %param.6) | data formatting | bytes 921600
  2.4 60.2 %shard_map.77 = (f32[3,300,128]{2,1,0:T(8,128)}, f32[3,300,128]{2,1,0:T(8,128)}) custom-call(f32[3,300,128]{2,1,0:T(8,128)} %bitcast.10, bf16[1800,1800]{1,0:T(8,128)(2,1)} %bitcast.9, bf16[24,1800]{1,0:T(8,128)(2,1)} %bitcast.14, bf16[6,300,300]{2,1,0:T(8,128)(2,1)} %bitcast.11, bf16[27,27]{1,0:T(8,128)(2,1)} %cinv_hbm.1, s32[8]{0:T(128)} %bitcast.15), custom_call_target="tpu_custom_call" | custom-call | tf_op jit(solution)/shard_map/pallas_call | solution.py:414
  62.7 2.3 %copy.8 = f32[1,1,1,3,300,128]{5,2,4,3,1,0:T(1,128)} copy(f32[1,1,1,3,300,128]{5,4,3,2,1,0:T(8,128)} %bitcast.13) | data formatting | bytes 921600
  64.9 2.3 %copy.9 = f32[1,1,1,3,300,128]{5,2,4,3,1,0:T(1,128)} copy(f32[1,1,1,3,300,128]{5,4,3,2,1,0:T(8,128)} %bitcast.12) | data formatting | bytes 921600

commit v2 on v1

--- a/solution.py
+++ b/solution.py
@@ -75,7 +75,6 @@
     total = faces * width
     ncq = c_own.shape[1]
     wide = c_own.shape[2]
-    prow = coarse_a.shape[2]
     here = [lax.axis_index(name) for name in AXES]
     plane = nx * ny
     me_plane = here[0] * ny + here[1]
@@ -98,6 +97,12 @@
     def z_peer(offset):
         return {"gz": lax.rem(here[2] + offset, nz)}
 
+    barrier = pltpu.get_barrier_semaphore()
+    for offset in range(1, plane):
+        pl.semaphore_signal(barrier, inc=1, device_id=plane_peer(offset), device_id_type=MESH)
+    for offset in range(1, nz):
+        pl.semaphore_signal(barrier, inc=1, device_id=z_peer(offset), device_id_type=MESH)
+
     loads = []
     for index, (src, dst) in enumerate(
         ((rhs_hbm, rhs_v), (coup_hbm, coup_v), (cinv_hbm, cinv_v), (stiff_hbm, k_own), (flex_hbm, flex_v))
@@ -106,6 +111,51 @@
         copy.start()
         loads.append(copy)
 
+    loads[0].wait()
+    for axis in range(3):
+        owned = rhs_v[axis, :, 0, :] * masks[2 * axis + 1]
+        res_v[2 * axis + 1] = owned
+        r_send[axis] = owned.astype(BF16)
+    pl.semaphore_wait(barrier, plane - 1 + nz - 1)
+
+    def remote(src, dst, send_sem, recv_sem, target):
+        return pltpu.make_async_remote_copy(
+            src_ref=src, dst_ref=dst, send_sem=send_sem, recv_sem=recv_sem, device_id=target, device_id_type=MESH
+        )
+
+    def rhs_copy(axis):
+        return remote(
+            r_send.at[axis], r_recv.at[axis], setup_send.at[0, 2 * axis + 1], setup_recv.at[0, 2 * axis],
+            neighbour(2 * axis + 1),
+        )
+
+    def k_copy(face):
+        return remote(
+            k_own.at[face], k_nb.at[face ^ 1], setup_send.at[1, face], setup_recv.at[1, face ^ 1], neighbour(face)
+        )
+
+    def c_copy(face):
+        return remote(
+            c_own.at[face], c_nb.at[face ^ 1], setup_send.at[2, face], setup_recv.at[2, face ^ 1], neighbour(face)
+        )
+
+    def halo_copy(it, face):
+        return remote(
+            img_send.at[it, face], img_recv.at[it, face ^ 1], halo_send.at[it, face], halo_recv.at[it, face ^ 1],
+            neighbour(face),
+        )
+
+    def when_has(face, action):
+        @pl.when(has[face])
+        def _():
+            action()
+
+    for axis in (2, 0, 1):
+        when_has(2 * axis + 1, lambda axis=axis: rhs_copy(axis).start())
+    loads[3].wait()
+    for face in (4, 0, 2, 5, 1, 3):
+        when_has(face, lambda face=face: k_copy(face).start())
+
     for face in range(faces):
 
         @pl.when(jnp.logical_not(has[face]))
@@ -120,54 +170,6 @@
         @pl.when(jnp.logical_not(has[2 * axis]))
         def _(axis=axis):
             r_recv[axis] = jnp.zeros((width, cols), BF16)
-
-    barrier = pltpu.get_barrier_semaphore()
-    for offset in range(1, plane):
-        pl.semaphore_signal(barrier, inc=1, device_id=plane_peer(offset), device_id_type=MESH)
-    for offset in range(1, nz):
-        pl.semaphore_signal(barrier, inc=1, device_id=z_peer(offset), device_id_type=MESH)
-
-    loads[0].wait()
-    for axis in range(3):
-        r_send[axis] = (rhs_v[axis] * masks[2 * axis + 1]).astype(BF16)
-    pl.semaphore_wait(barrier, plane - 1 + nz - 1)
-
-    def remote(src, dst, send_sem, recv_sem, target):
-        return pltpu.make_async_remote_copy(
-            src_ref=src, dst_ref=dst, send_sem=send_sem, recv_sem=recv_sem, device_id=target, device_id_type=MESH
-        )
-
-    def rhs_copy(axis):
-        return remote(
-            r_send.at[axis], r_recv.at[axis], setup_send.at[0, 2 * axis + 1], setup_recv.at[0, 2 * axis],
-            neighbour(2 * axis + 1),
-        )
-
-    def k_copy(face):
-        return remote(
-            stiff_hbm.at[face], k_nb.at[face ^ 1], setup_send.at[1, face], setup_recv.at[1, face ^ 1], neighbour(face)
-        )
-
-    def c_copy(face):
-        return remote(
-            c_own.at[face], c_nb.at[face ^ 1], setup_send.at[2, face], setup_recv.at[2, face ^ 1], neighbour(face)
-        )
-
-    def halo_copy(it, face):
-        return remote(
-            img_send.at[it, face], img_recv.at[it, face ^ 1], halo_send.at[it, face], halo_recv.at[it, face ^ 1],
-            neighbour(face),
-        )
-
-    def when_has(face, action):
-        @pl.when(has[face])
-        def _():
-            action()
-
-    for axis in (2, 0, 1):
-        when_has(2 * axis + 1, lambda axis=axis: rhs_copy(axis).start())
-    for face in (4, 0, 2, 5, 1, 3):
-        when_has(face, lambda face=face: k_copy(face).start())
 
     loads[1].wait()
     lane = lax.broadcasted_iota(jnp.int32, (1, 3 * corners), 1)
@@ -198,22 +200,20 @@
     for axis in range(3):
         when_has(2 * axis, lambda axis=axis: rhs_copy(axis).wait_recv())
         res_v[2 * axis] = -r_recv[axis].astype(F32)
-        res_v[2 * axis + 1] = rhs_v[axis] * masks[2 * axis + 1]
     loads[2].wait()
-    loads[3].wait()
-
-    coarse_row = lax.broadcasted_iota(jnp.int32, (prow, cols), 0)
+
+    scalar_row = lax.broadcasted_iota(jnp.int32, (8, cols), 0)
     rho_now = None
     step_size = None
     for it in range(ITERS):
         last = it + 1 == ITERS
         rho_acc = jnp.zeros((1, cols), F32)
+        if it == 0:
+            for face in range(faces):
+                when_has(face, lambda face=face: remote(
+                    k_own.at[face], k_nb.at[face], setup_send.at[1, face], setup_recv.at[1, face], neighbour(face)
+                ).wait_recv())
         for face in range(faces):
-            if it == 0:
-                when_has(face, lambda face=face: k_copy(face).wait_send())
-                when_has(face, lambda face=face: remote(
-                    stiff_hbm.at[face], k_nb.at[face], setup_send.at[1, face], setup_recv.at[1, face], neighbour(face)
-                ).wait_recv())
             res = res_v[face]
             half = (0.5 * res).astype(BF16)
             z = jnp.dot(k_own[face], half, preferred_element_type=F32)
@@ -228,9 +228,7 @@
         if it == 0:
             loads[4].wait()
         coarse_part = jnp.dot(casm_v[...], signed, preferred_element_type=F32)
-        if prow > ncq:
-            coarse_part = jnp.concatenate([coarse_part, jnp.zeros((prow - ncq, cols), F32)], axis=0)
-        coarse_a[it, 0] = jnp.where(coarse_row == ncoarse, rho_acc, coarse_part[0:prow])
+        coarse_a[it, 0] = coarse_part.astype(BF16)
 
         def a_copy(offset, it=it):
             return remote(
@@ -260,26 +258,29 @@
             a_copy(offset).start()
 
         energy_acc = jnp.zeros((8, cols), F32)
-        begin = 0
-        for face in range(faces):
-            end = total if face + 1 == faces else round_up((face + 1) * width, 16)
+        cuts = [0] + [round_up(2 * a * width, 16) for a in range(1, faces // 2)] + [total]
+        order = [faces // 2 - 1] + list(range(faces // 2 - 1))
+        for position, axis in enumerate(order):
+            begin, end = cuts[axis], cuts[axis + 1]
             image = jnp.dot(flex_v[begin:end, :], signed_v[...], preferred_element_type=F32)
             imgflat[begin:end, :] = image
             weighted = image * signed_v[begin:end, :].astype(F32)
             energy_acc = energy_acc + jnp.sum(weighted.reshape(-1, 8, cols), axis=0)
-            begin = end
-            img_send[it, face] = imgflat[face * width : (face + 1) * width, :].astype(BF16)
-            if not last or face % 2 == 0:
-                when_has(face, lambda face=face, it=it: halo_copy(it, face).start())
-        energy_a[it, 0] = energy_acc
+            for face in (2 * axis, 2 * axis + 1):
+                img_send[it, face] = imgflat[face * width : (face + 1) * width, :].astype(BF16)
+            for face in (2 * axis, 2 * axis + 1):
+                if not last or face % 2 == 0:
+                    when_has(face, lambda face=face, it=it: halo_copy(it, face).start())
+        energy_row = jnp.sum(energy_acc, axis=0, keepdims=True)
+        energy_a[it, 0] = jnp.where(scalar_row == 0, energy_row, jnp.where(scalar_row == 1, rho_acc, 0.0))
         for offset in range(1, plane):
             ea_copy(offset).start()
 
-        part = coarse_a[it, 0]
+        part = coarse_a[it, 0].astype(F32)
         for offset in range(1, plane):
             a_copy(offset).wait_recv()
-            part = part + coarse_a[it, offset]
-        coarse_b[it, 0] = part
+            part = part + coarse_a[it, offset].astype(F32)
+        coarse_b[it, 0] = part.astype(BF16)
         for offset in range(1, nz):
             b_copy(offset).start()
         energy = energy_a[it, 0]
@@ -300,17 +301,10 @@
                 stack = jnp.concatenate([own, -other] * (corr_v.shape[2] // (2 * ncq)), axis=0)
                 corr_v[face] = stack.T[0:width].astype(BF16)
 
-        coarse = coarse_b[it, 0]
+        coarse = part
         for offset in range(1, nz):
             b_copy(offset).wait_recv()
-            coarse = coarse + coarse_b[it, offset]
-        rho = jnp.sum(jnp.where(coarse_row == ncoarse, coarse, 0.0), axis=0, keepdims=True)
-        if prow > ncq:
-            coarse = coarse[0:ncq]
-        elif prow < ncq:
-            coarse = jnp.concatenate([coarse, jnp.zeros((ncq - prow, cols), F32)], axis=0)
-        rows_q = lax.broadcasted_iota(jnp.int32, (ncq, cols), 0)
-        coarse = jnp.where(rows_q < ncoarse, coarse, 0.0)
+            coarse = coarse + coarse_b[it, offset].astype(F32)
         sol = jnp.dot(cinv_v[...], coarse[0:ncoarse].astype(BF16), preferred_element_type=F32)
         sol = jnp.concatenate([sol, jnp.zeros((ncq - ncoarse, cols), F32)], axis=0) if ncq > ncoarse else sol
         sol_hi = sol.astype(BF16)
@@ -325,7 +319,8 @@
         for offset in range(1, nz):
             eb_copy(offset).wait_recv()
             energy = energy + energy_b[it, offset]
-        energy = jnp.sum(energy, axis=0, keepdims=True) + coarse_energy
+        rho = energy[1:2]
+        energy = energy[0:1] + coarse_energy
 
         if it == 0:
             step_size = rho / energy
@@ -342,6 +337,9 @@
                 img_send.at[it, face], img_recv.at[it, face], halo_send.at[it, face], halo_recv.at[it, face],
                 neighbour(face),
             ).wait_recv())
+        for face in range(faces):
+            if last and face % 2 == 0:
+                continue
             image = img_send[it, face].astype(F32) - img_recv[it, face].astype(F32)
             for piece in sol_parts:
                 image = image + jnp.dot(corr_v[face], piece, preferred_element_type=F32)
@@ -350,7 +348,7 @@
                 image = image + beta * s_v[face]
             new_res = res_v[face] - step_size * image
             if last:
-                resid_ref[face // 2] = new_res
+                resid_ref[face // 2, :, 0, :] = new_res
             else:
                 s_v[face] = image
                 res_v[face] = new_res
@@ -365,13 +363,14 @@
                 if it > 0:
                     moved = moved + lam_v[axis]
                 if last:
-                    mult_ref[axis] = moved
+                    mult_ref[axis, :, 0, :] = moved
                 else:
                     lam_v[axis] = moved
 
     for axis in range(3):
         when_has(2 * axis + 1, lambda axis=axis: rhs_copy(axis).wait_send())
     for face in range(faces):
+        when_has(face, lambda face=face: k_copy(face).wait_send())
         when_has(face, lambda face=face: c_copy(face).wait_send())
         for it in range(ITERS):
             if it + 1 < ITERS or face % 2 == 0:
@@ -390,18 +389,17 @@
 
 
 def body(sizes, dual_rhs, local_flex, corner_coupling, face_stiffness, coarse_inverse, corner_ids):
-    rhs = dual_rhs[0, 0, 0]
+    rhs = dual_rhs.reshape(dual_rhs.shape[3:5] + (1,) + dual_rhs.shape[5:])
     flex = local_flex[0, 0, 0]
     coupling = corner_coupling[0, 0, 0]
     stiffness = face_stiffness[0, 0, 0]
     ids = corner_ids[0, 0, 0]
     faces, width, _ = stiffness.shape
-    cols = rhs.shape[2]
+    cols = rhs.shape[3]
     ncoarse = coarse_inverse.shape[0]
     corners = ids.shape[0]
     total = faces * width
     ncq = round_up(ncoarse, 32)
-    prow = round_up(ncoarse + 1, 8)
     wide = round_up(width, 128)
     span = round_up((faces - 1) * width // 128 * 128 + max(round_up(width + 127, 128), wide), 128)
     nx, ny, nz = sizes
@@ -440,8 +438,8 @@
             pltpu.VMEM((3, width, cols), F32),
             pltpu.VMEM((faces, width, cols), F32),
             pltpu.VMEM((3, width, cols), F32),
-            pltpu.VMEM((ITERS, plane, prow, cols), F32),
-            pltpu.VMEM((ITERS, nz, prow, cols), F32),
+            pltpu.VMEM((ITERS, plane, ncq, cols), BF16),
+            pltpu.VMEM((ITERS, nz, ncq, cols), BF16),
             pltpu.VMEM((ITERS, plane, 8, cols), F32),
             pltpu.VMEM((ITERS, nz, 8, cols), F32),
             dma((5,)),
@@ -462,7 +460,7 @@
             collective_id=0, has_side_effects=True, vmem_limit_bytes=62 * 1024 * 1024
         ),
     )(rhs, flex, coupling, stiffness, coarse_inverse, ids)
-    return (mult[None, None, None], resid[None, None, None])
+    return (mult.reshape(dual_rhs.shape), resid.reshape(dual_rhs.shape))
 
 
 def solution(mesh):

time: 67.4 us -> 61.4 us (0.911)
  Pallas kernels: 60.2 us -> 56.9 us
  local copies, waits for them, and re-layouts: 6.35 us -> 3.64 us
    pallas_call x1, Pallas kernels: 60.2 us -> 56.9 us  [body(): pl.pallas_call(functools.partial(kernel, sizes, (faces, width, cols, ncoa...]
    unnamed x3 -> x2, local copies, waits for them, and re-layouts: 6.35 us -> 3.64 us
where the time goes in v2:
time: 61.4 us; the launch traced here: 61.2 us
  Pallas kernels  56.9 us (93%)
  local copies, waits for them, and re-layouts  3.64 us (6%)
  between operations  0.64 us (1%)
    pallas_call x1, Pallas kernels, body(): pl.pallas_call(functools.partial(kernel, sizes, (faces, width, cols, ncoa...  56.9 us
    unnamed x2, local copies, waits for them, and re-layouts  3.64 us

profile of v2, /device:TPU:0, one launch (start us, length us, event | category | flops | bytes accessed | tf_op | source)
XLA Modules:
  0.0 61.2 jit_solution(7931083957333910912)
XLA Ops:
  0.6 56.9 %shard_map.77 = (f32[3,300,1,128]{3,2,1,0:T(1,128)}, f32[3,300,1,128]{3,2,1,0:T(1,128)}) custom-call(f32[3,300,1,128]{3,2,1,0:T(1,128)} %bitcast.15, bf16[1800,1800]{1,0:T(8,128)(2,1)} %bitcast.11, bf16[24,1800]{1,0:T(8,128)(2,1)} %bitcast.16, bf16[6,300,300]{2,1,0:T(8,128)(2,1)} %bitcast.12, bf16[27,27]{1,0:T(8,128)(2,1)} %cinv_hbm.1, s32[8]{0:T(128)} %bitcast.17), custom_call_target="tpu_custom_call" | custom-call | tf_op jit(solution)/shard_map/pallas_call | solution.py:412
  57.6 1.8 %copy.12 = f32[1,1,1,3,300,128]{5,2,4,3,1,0:T(1,128)} copy(f32[1,1,1,3,300,128]{5,2,4,3,1,0:T(1,128)} %bitcast.14) | data formatting | bytes 921600
  59.4 1.8 %copy.13 = f32[1,1,1,3,300,128]{5,2,4,3,1,0:T(1,128)} copy(f32[1,1,1,3,300,128]{5,2,4,3,1,0:T(1,128)} %bitcast.13) | data formatting | bytes 921600
